TPU v7x, 32 devices: a whole 2x2x4 slice. The times are simulated.
32 devices in a mesh: seq: 8 (over z, y), head: 4 (over x, core).
Axes of the slice: x: 2, y: 2, z: 4, core: 2. Of those that a mesh axis runs over, the one named last changes fastest.
Arguments:
- q_low: bfloat16 [2048, 1536], P('seq', 'head'), may hold values from -500 to 500
- q_gain: bfloat16 [1536], P('head'), may hold values from 0.099609375 to 1.8984375
- q_up: bfloat16 [1536, 24576], P(None, 'head'), may hold values from -0.15625 to 0.15625
- key_absorb: bfloat16 [128, 128, 512], P('head'), may hold values from -0.5 to 0.5
- value_absorb: bfloat16 [128, 512, 128], P('head'), may hold values from -0.25 to 0.25
- latent_cache: bfloat16 [65536, 576], P('seq'), may hold values from -1300 to 1300
- tile_picks: int32 [16, 16], P('seq'), may hold values from 0 to 511, as said below
Outputs:
- attended: bfloat16 [2048, 16384], P('seq', 'head')
Inputs may be any that keep to these rules, and one draw needn't show every extreme that they name: `tile_picks`: the 16 tiles of one query block differ. Of all tiles that the query blocks of one index of seq select together, at most 8 lie in the cache rows of one index of seq, and exactly 8 in those of some index.
All inputs are finite; a program needn't handle non-finite values.
Results may differ from a plain program's by a relative error of at most 0.03.
Values may be sent and summed in bfloat16 or wider, within the bound.
A program may use at most 192 MiB of HBM per device.

v0:
```python
import jax
import jax.numpy as jnp
from jax import lax
from jax.sharding import PartitionSpec as P

NOPE = 128
ROPE = 64
LATENT = 512
VDIM = 128
TILE = 128
TOPT = 16
QBLK = 128


def rms_normed(q_low, q_gain):
    values = q_low.astype(jnp.float32)
    power = jnp.mean(values * values, axis=-1, keepdims=True)
    return (values * lax.rsqrt(power + 1e-06) * q_gain.astype(jnp.float32)).astype(jnp.bfloat16)


def rotate(rope, positions):
    half = rope.shape[-1] // 2
    freq = jnp.power(
        jnp.float32(10000.0), -(2.0 * jnp.arange(half, dtype=jnp.float32)) / rope.shape[-1]
    )
    angle = positions.astype(jnp.float32)[:, None] * freq[None, :]
    cosine = jnp.cos(angle)[:, None, :]
    sine = jnp.sin(angle)[:, None, :]
    first = rope[..., :half].astype(jnp.float32)
    second = rope[..., half:].astype(jnp.float32)
    return jnp.concatenate(
        [first * cosine - second * sine, first * sine + second * cosine], axis=-1
    ).astype(jnp.bfloat16)


def owner_rank(picks, tiles_dev):
    owner = picks // tiles_dev
    order = jnp.arange(picks.shape[0], dtype=jnp.int32)
    before = (owner[:, None] == owner[None, :]) & (order[None, :] < order[:, None])
    return (owner, jnp.sum(before.astype(jnp.int32), axis=1))


def place_table(place, local, length):
    hit = place[:, None] == jnp.arange(length, dtype=jnp.int32)[None, :]
    return jnp.sum(jnp.where(hit, local[:, None], 0), axis=0)


def body(q_low, q_gain, q_up, key_absorb, value_absorb, latent_cache, tile_picks):
    whole_low, whole_gain = (
        lax.all_gather(q_low, "head", axis=1, tiled=True),
        lax.all_gather(q_gain, "head", axis=0, tiled=True),
    )
    rows = whole_low.shape[0]
    group = key_absorb.shape[0]
    width = latent_cache.shape[1]
    seq_count = lax.axis_size("seq")
    tiles_dev = latent_cache.shape[0] // TILE
    picks = tile_picks.reshape(-1)
    count = picks.shape[0]
    cap = max(2, 2 * count // seq_count)
    owner, rank = owner_rank(picks, tiles_dev)
    cache_tiles = latent_cache.reshape(tiles_dev, TILE, width)
    share = TILE // lax.axis_size("head")
    cache_tiles = lax.dynamic_slice_in_dim(cache_tiles, lax.axis_index("head") * share, share, 1)
    requests = place_table(owner * cap + rank, picks % tiles_dev, seq_count * cap).reshape(
        seq_count, cap
    )
    serve_requests = lax.all_to_all(requests, "seq", split_axis=0, concat_axis=0, tiled=True)
    found = jnp.take(cache_tiles, serve_requests, axis=0)
    fetched = lax.all_to_all(found, "seq", split_axis=0, concat_axis=0, tiled=True)
    flat = fetched.reshape(seq_count * cap, fetched.shape[2], width)
    keys = jnp.take(flat, owner * cap + rank, axis=0)
    keys = lax.all_gather(keys, "head", axis=1, tiled=True)
    keys = keys.reshape(count // TOPT, TOPT * TILE, width)
    normed = rms_normed(whole_low, whole_gain)
    query = jnp.dot(normed, q_up, preferred_element_type=jnp.float32).astype(jnp.bfloat16)
    query = query.reshape(rows, group, NOPE + ROPE)
    context = latent_cache.shape[0] * seq_count
    positions = context + lax.axis_index("seq") * rows + jnp.arange(rows, dtype=jnp.int32)
    rotated = rotate(query[..., NOPE:], positions)
    latent_q = jnp.einsum(
        "thn,hnl->thl", query[..., :NOPE], key_absorb, preferred_element_type=jnp.float32
    ).astype(jnp.bfloat16)
    full_q = jnp.concatenate([latent_q, rotated], axis=-1).reshape(
        count // TOPT, QBLK * group, width
    )
    scale = float(NOPE + ROPE) ** (-0.5)

    def one_block(operands):
        block_q, block_keys = operands
        scores = (
            lax.dot_general(
                block_q, block_keys, (((1,), (1,)), ((), ())), preferred_element_type=jnp.float32
            )
            * scale
        )
        weights = jax.nn.softmax(scores, axis=-1).astype(jnp.bfloat16)
        return jnp.dot(weights, block_keys[:, :LATENT], preferred_element_type=jnp.float32).astype(
            jnp.bfloat16
        )

    mixed = lax.map(one_block, (full_q, keys)).reshape(rows, group, LATENT)
    attended = jnp.einsum("thl,hlv->thv", mixed, value_absorb, preferred_element_type=jnp.float32)
    return attended.astype(jnp.bfloat16).reshape(rows, group * VDIM)


def solution(mesh):
    in_specs = (
        P("seq", "head"),
        P("head"),
        P(None, "head"),
        P("head", None, None),
        P("head", None, None),
        P("seq", None),
        P("seq", None),
    )
    out_specs = P("seq", "head")
    return jax.shard_map(body, mesh=mesh, in_specs=in_specs, out_specs=out_specs, check_vma=False)
```

profile of v0, /device:TPU:0, one launch (start us, length us, event | category | flops | bytes accessed | tf_op | source)
XLA Modules:
  0.0 304.3 jit_solution(13812923504323022759)
XLA Ops:
  8.3 7.3 %all-to-all-start = ((s32[8,1,8]{2,1,0:T(1,128)}), s32[8,1,8]{2,1,0:T(1,128)S(1)}, u32[]{:S(2)}, u32[]{:S(2)}) async-start(s32[8,1,8]{2,1,0:T(1,128)} %bitcast.6), calls=%async_computation | async-start | bytes 8192 | tf_op jit(solution)/shard_map/all_to_all | solution.py:68
  15.6 14.1 %copy.49 = bf16[8192,576]{1,0:T(8,128)(2,1)} copy(bf16[8192,576]{0,1:T(8,128)(2,1)} %param.14) | data formatting | bytes 18874368 | tf_op args[5]
  34.1 3.6 %broadcast_select_fusion = bf16[8,8,32,576]{3,2,1,0:T(8,128)(2,1)} fusion(bf16[8,8,32,576]{3,2,1,0:T(8,128)(2,1)} %bitcast.53, pred[8,8]{1,0:T(8,128)(4,1)S(1)} %compare_and_fusion), kind=kLoop, calls=%fused_computation.22 | loop fusion | flops 1179648 | bytes 4718656 | tf_op jit(solution)/shard_map/jit(_take)/select_n | solution.py:69
  37.8 6.1 %all-to-all-start.1 = ((bf16[8,8,32,576]{3,2,1,0:T(8,128)(2,1)}), bf16[8,8,32,576]{3,2,1,0:T(8,128)(2,1)S(1)}, u32[]{:S(2)}, u32[]{:S(2)}) async-start(bf16[8,8,32,576]{3,2,1,0:T(8,128)(2,1)} %broadcast_select_fusion), calls=%async_computation.1 | async-start | bytes 5242880 | tf_op jit(solution)/shard_map/all_to_all | solution.py:70
  44.0 58.8 %all-to-all-done.1 = bf16[8,8,32,576]{3,2,1,0:T(8,128)(2,1)S(1)} async-done(((bf16[8,8,32,576]{3,2,1,0:T(8,128)(2,1)}), bf16[8,8,32,576]{3,2,1,0:T(8,128)(2,1)S(1)}, u32[]{:S(2)}, u32[]{:S(2)}) %all-to-all-start.1) | async-done | bytes 2359328 | tf_op jit(solution)/shard_map/all_to_all | solution.py:70
  104.5 2.6 broadcast_select_fusion.1
  107.2 5.2 %all-gather = bf16[4,1,384]{2,1,0:T(2,128)(2,1)S(1)} all-gather(bf16[1,1,384]{2,1,0:T(2,128)(2,1)S(1)} %reshape.325), channel_id=1, replica_groups=mesh['seq'=8,'head'=4] {'head'}, dimensions={0}, use_global_device_ids=true | all-gather | bytes 3840 | tf_op jit(solution)/shard_map/all_gather | solution.py:51
  112.4 12.5 %all_gather.9 = bf16[256,1536]{1,0:T(8,128)(2,1)S(1)} all-gather(bf16[256,384]{1,0:T(8,128)(2,1)S(1)} %copy-done.3), channel_id=1, replica_groups=mesh['seq'=8,'head'=4] {'head'}, dimensions={1}, use_global_device_ids=true | all-gather | bytes 983040 | tf_op jit(solution)/shard_map/all_gather | solution.py:50
  125.2 13.1 %convolution_convert_fusion = bf16[256,6144]{1,0:T(8,128)(2,1)} fusion(bf16[1536,6144]{1,0:T(8,128)(2,1)} %param.11, bf16[256,1536]{1,0:T(8,128)(2,1)S(1)} %all_gather.9, f32[1536]{0:T(1024)S(1)} %reshape.327, f32[256]{0:T(256)S(1)} %add_rsqrt_fusion), kind=kOutput, calls=%fused_computation.21 | convolution fusion | flops 4834983936 | bytes 22813696 | tf_op jit(solution)/shard_map/dot_general | solution.py:76
  138.2 3.2 %copy.43 = bf16[256,6144]{0,1:T(8,128)(2,1)S(1)} copy(bf16[256,6144]{1,0:T(8,128)(2,1)} %convolution_convert_fusion) | data formatting | bytes 6291456 | tf_op jit(solution)/shard_map/convert_element_type | solution.py:76
  143.0 2.7 copy.45
  145.7 2.6 copy.46
  148.3 4.8 %convert_bitcast_fusion = bf16[256,32,512]{2,0,1:T(8,128)(2,1)S(1)} fusion(bf16[32,128,512]{2,1,0:T(8,128)(2,1)} %param.12, bf16[256,32,192]{0,2,1:T(8,128)(2,1)S(1)} %bitcast.51), kind=kOutput, calls=%fused_computation.20 | convolution fusion | flops 1077936128 | bytes 14680064 | tf_op jit(solution)/shard_map/thn,hnl->thl/dot_general | solution.py:81
  153.1 12.0 %pad_maximum_fusion = bf16[256,32,576]{2,0,1:T(8,128)(2,1)} fusion(bf16[256,32,32]{2,0,1:T(8,128)(2,1)S(1)} %copy-done.2, bf16[256,32,32]{2,0,1:T(8,128)(2,1)S(1)} %copy-done.1, bf16[256,32,512]{2,0,1:T(8,128)(2,1)S(1)} %convert_bitcast_fusion), kind=kLoop, calls=%fused_computation.17 | loop fusion | flops 28311552 | bytes 18874368 | tf_op jit(solution)/shard_map/concatenate | solution.py:84
  165.1 14.0 %copy.47 = bf16[256,32,576]{2,1,0:T(8,128)(2,1)} copy(bf16[256,32,576]{2,0,1:T(8,128)(2,1)} %pad_maximum_fusion) | data formatting | bytes 18874368 | tf_op jit(solution)/shard_map/concatenate | solution.py:84
  179.1 105.8 %while.10 = (s32[]{:T(128)}, bf16[2,4096,512]{2,1,0:T(8,128)(2,1)}, bf16[2,4096,576]{2,1,0:T(8,128)(2,1)}, bf16[2,2048,576]{2,1,0:T(8,128)(2,1)}, s32[]{:T(128)}) while((s32[]{:T(128)}, bf16[2,4096,512]{2,1,0:T(8,128)(2,1)}, bf16[2,4096,576]{2,1,0:T(8,128)(2,1)}, bf16[2,2048,576]{2,1,0:T(8,128)(2,1)}, s32[]{:T(128)}) %tuple.31), condition=%wide.region_6.7_spmd, body=%wide.region_3.6_spmd.sunk | while | flops 18331197440 | bytes 138495600 | solution.py:102
  179.1 22.0 %multiply_reduce_fusion.2 = (f32[4096]{0:T(1024)S(1)}, f32[4096,2048]{0,1:T(8,128)}) fusion(bf16[2,2048,576]{2,1,0:T(8,128)(2,1)} %get-tuple-element.88, s32[]{:T(128)} %get-tuple-element.80, bf16[2,4096,576]{2,1,0:T(8,128)(2,1)} %get-tuple-element.87), kind=kOutput, calls=%fused_computation.4.clone.1 | convolution fusion | flops 9680449536 | bytes 41436160 | tf_op jit(solution)/shard_map/while/body/eval_jaxpr/dot_general | solution.py:92
  201.1 14.0 %fusion.36 = f32[4096]{0:T(1024)S(1)} fusion(f32[4096,2048]{0,1:T(8,128)} %get-tuple-element.73, f32[4096]{0:T(1024)S(1)} %get-tuple-element.74), kind=kLoop, calls=%fused_computation.5.clone.1 | loop fusion | flops 25161728 | bytes 33587200 | tf_op jit(solution)/shard_map/while/body/eval_jaxpr/reduce_sum | solution.py:97
  215.4 16.6 %fusion.37 = bf16[2,4096,512]{2,1,0:T(8,128)(2,1)} fusion(bf16[2,4096,512]{2,1,0:T(8,128)(2,1)} %get-tuple-element.81, s32[]{:T(128)} %get-tuple-element.80, f32[4096,2048]{0,1:T(8,128)} %get-tuple-element.73, f32[4096]{0:T(1024)S(1)} %fusion.36, f32[4096]{0:T(1024)S(1)} %get-tuple-element.74, bf16[2048,576]{1,0:T(8,128)(2,1)S(1)} %dynamic-slice_bitcast_fusion.3), kind=kOutput, calls=%fused_computation.9.clone.1 | convolution fusion | flops 8625586176 | bytes 39879168 | tf_op jit(solution)/shard_map/while/body/eval_jaxpr/dot_general | solution.py:98
  232.0 22.0 %multiply_reduce_fusion.2 = (f32[4096]{0:T(1024)S(1)}, f32[4096,2048]{0,1:T(8,128)}) fusion(bf16[2,2048,576]{2,1,0:T(8,128)(2,1)} %get-tuple-element.88, s32[]{:T(128)} %get-tuple-element.80, bf16[2,4096,576]{2,1,0:T(8,128)(2,1)} %get-tuple-element.87), kind=kOutput, calls=%fused_computation.4.clone.1 | convolution fusion | flops 9680449536 | bytes 41436160 | tf_op jit(solution)/shard_map/while/body/eval_jaxpr/dot_general | solution.py:92
  254.0 14.0 %fusion.36 = f32[4096]{0:T(1024)S(1)} fusion(f32[4096,2048]{0,1:T(8,128)} %get-tuple-element.73, f32[4096]{0:T(1024)S(1)} %get-tuple-element.74), kind=kLoop, calls=%fused_computation.5.clone.1 | loop fusion | flops 25161728 | bytes 33587200 | tf_op jit(solution)/shard_map/while/body/eval_jaxpr/reduce_sum | solution.py:97
  268.3 16.6 %fusion.37 = bf16[2,4096,512]{2,1,0:T(8,128)(2,1)} fusion(bf16[2,4096,512]{2,1,0:T(8,128)(2,1)} %get-tuple-element.81, s32[]{:T(128)} %get-tuple-element.80, f32[4096,2048]{0,1:T(8,128)} %get-tuple-element.73, f32[4096]{0:T(1024)S(1)} %fusion.36, f32[4096]{0:T(1024)S(1)} %get-tuple-element.74, bf16[2048,576]{1,0:T(8,128)(2,1)S(1)} %dynamic-slice_bitcast_fusion.3), kind=kOutput, calls=%fused_computation.9.clone.1 | convolution fusion | flops 8625586176 | bytes 39879168 | tf_op jit(solution)/shard_map/while/body/eval_jaxpr/dot_general | solution.py:98
  284.9 9.7 %fusion.14 = bf16[32,256,128]{1,2,0:T(8,128)(2,1)S(1)} fusion(bf16[32,512,128]{2,1,0:T(8,128)(2,1)} %param.13, bf16[256,32,512]{2,1,0:T(8,128)(2,1)} %bitcast.58), kind=kOutput, calls=%fused_computation.26 | convolution fusion | flops 1074790400 | bytes 14680064 | tf_op jit(solution)/shard_map/thl,hlv->thv/dot_general | solution.py:103
  294.6 2.9 copy.52
  (46 shorter events, 10.4 us)
Async XLA Ops:
  8.3 23.4 %all-to-all-start = ((s32[8,1,8]{2,1,0:T(1,128)}), s32[8,1,8]{2,1,0:T(1,128)S(1)}, u32[]{:S(2)}, u32[]{:S(2)}) async-start(s32[8,1,8]{2,1,0:T(1,128)} %bitcast.6), calls=%async_computation | async-start | bytes 8192 | tf_op jit(solution)/shard_map/all_to_all | solution.py:68
  34.1 9.8 %copy-start.5 = (s32[2,16]{1,0:T(2,128)S(1)}, s32[2,16]{1,0:T(2,128)}, u32[]{:S(2)}) copy-start(s32[2,16]{1,0:T(2,128)} %param.15) | copy-start | bytes 388
  37.7 69.4 %copy-start.4 = (bf16[384]{0:T(512)(128)(2,1)S(1)}, bf16[384]{0:T(512)(128)(2,1)}, u32[]{:S(2)}) copy-start(bf16[384]{0:T(512)(128)(2,1)} %param.10) | copy-start | bytes 2308
  37.8 74.7 %copy-start.3 = (bf16[256,384]{1,0:T(8,128)(2,1)S(1)}, bf16[256,384]{1,0:T(8,128)(2,1)}, u32[]{:S(2)}) copy-start(bf16[256,384]{1,0:T(8,128)(2,1)} %param.9) | copy-start | bytes 589828
  37.8 65.0 %all-to-all-start.1 = ((bf16[8,8,32,576]{3,2,1,0:T(8,128)(2,1)}), bf16[8,8,32,576]{3,2,1,0:T(8,128)(2,1)S(1)}, u32[]{:S(2)}, u32[]{:S(2)}) async-start(bf16[8,8,32,576]{3,2,1,0:T(8,128)(2,1)} %broadcast_select_fusion), calls=%async_computation.1 | async-start | bytes 5242880 | tf_op jit(solution)/shard_map/all_to_all | solution.py:70
  43.9 135.3 %all-gather.3.cloned.1.call-start = ((), (), s32[]{:S(2)}) async-start(), calls=%async_computation.2 | async-start | bytes 6553600 | tf_op jit(solution)/shard_map/all_gather | solution.py:73
  148.3 4.8 %copy-start.1 = (bf16[256,32,32]{2,0,1:T(8,128)(2,1)S(1)}, bf16[256,32,32]{2,0,1:T(8,128)(2,1)}, u32[]{:S(2)}) copy-start(bf16[256,32,32]{2,0,1:T(8,128)(2,1)} %copy.45) | copy-start | bytes 1572868
  148.3 4.8 %copy-start.2 = (bf16[256,32,32]{2,0,1:T(8,128)(2,1)S(1)}, bf16[256,32,32]{2,0,1:T(8,128)(2,1)}, u32[]{:S(2)}) copy-start(bf16[256,32,32]{2,0,1:T(8,128)(2,1)} %copy.46) | copy-start | bytes 1572868
  201.1 14.0 %copy-start = (bf16[2,2048,576]{2,1,0:T(8,128)(2,1)S(1)}, bf16[2,2048,576]{2,1,0:T(8,128)(2,1)}, u32[]{:S(2)}) copy-start(bf16[2,2048,576]{2,1,0:T(8,128)(2,1)} %get-tuple-element.88) | copy-start | bytes 14155780 | tf_op jit(solution)/shard_map/while
  254.0 14.0 %copy-start = (bf16[2,2048,576]{2,1,0:T(8,128)(2,1)S(1)}, bf16[2,2048,576]{2,1,0:T(8,128)(2,1)}, u32[]{:S(2)}) copy-start(bf16[2,2048,576]{2,1,0:T(8,128)(2,1)} %get-tuple-element.88) | copy-start | bytes 14155780 | tf_op jit(solution)/shard_map/while
Sparse Core Ops, SparseCore 0:
  107.3 42.6 all-gather.2
where the time goes:
time: 305 us; the launch traced here: 304 us
  matrix products  105 us (34%)
  waiting for transfers between devices  58.8 us (19%)
  other arithmetic  48.4 us (16%)
  local copies, waits for them, and re-layouts  47.7 us (16%)
  blocking collectives  17.7 us (6%)
  starting transfers between devices  13.5 us (4%)
  between operations  13.5 us (4%)
    all_to_all x1, waiting for transfers between devices, body(): lax.all_to_all(found, 'seq', split_axis=0, concat_axis=0, tiled=True)  58.8 us
    dot_general x2, matrix products, one_block(): lax.dot_general(block_q, block_keys, (((1,), (1,)), ((), ())), preferred_...  44 us
    dot_general x2, matrix products, one_block(): jnp.dot(weights, block_keys[:, :LATENT], preferred_element_type=jnp.float32)  33.2 us
    reduce_sum x2, other arithmetic, one_block(): weights = jax.nn.softmax(scores, axis=-1).astype(jnp.bfloat16)  28 us
    unnamed x12, local copies, waits for them, and re-layouts  14.1 us
    concatenate x1, local copies, waits for them, and re-layouts, body(): jnp.concatenate([latent_q, rotated], axis=-1)  14 us
    dot_general x1, matrix products, body(): jnp.dot(normed, q_up, preferred_element_type=jnp.float32)  13.1 us
    all_gather x1, blocking collectives, body(): lax.all_gather(q_low, 'head', axis=1, tiled=True)  12.5 us
  transfers between devices with their start and end apart: 3, of which 1 were waited for; matrix products, arithmetic and copies ran while one was open for 23% of the time, Pallas kernels for 0%

commit v1 on v0

--- a/solution.py
+++ b/solution.py
@@ -10,6 +10,22 @@
 TILE = 128
 TOPT = 16
 QBLK = 128
+
+
+def swapped_with_each(value, axis, split, join):
+    ways, here = (lax.axis_size(axis), lax.axis_index(axis))
+    width = value.shape[split] // ways
+    lengths = list(value.shape)
+    lengths[split] = width
+    height = lengths[join]
+    lengths[join] = height * ways
+    full = jnp.zeros(lengths, value.dtype)
+    for mask in range(ways):
+        part = lax.dynamic_slice_in_dim(value, (here ^ mask) * width, width, axis=split)
+        if mask:
+            part = lax.ppermute(part, axis, [(d, d ^ mask) for d in range(ways)])
+        full = lax.dynamic_update_slice_in_dim(full, part, (here ^ mask) * height, axis=join)
+    return full
 
 
 def rms_normed(q_low, q_gain):
@@ -67,7 +83,7 @@
     )
     serve_requests = lax.all_to_all(requests, "seq", split_axis=0, concat_axis=0, tiled=True)
     found = jnp.take(cache_tiles, serve_requests, axis=0)
-    fetched = lax.all_to_all(found, "seq", split_axis=0, concat_axis=0, tiled=True)
+    fetched = swapped_with_each(found, "seq", 0, 0)
     flat = fetched.reshape(seq_count * cap, fetched.shape[2], width)
     keys = jnp.take(flat, owner * cap + rank, axis=0)
     keys = lax.all_gather(keys, "head", axis=1, tiled=True)

time: 305 us -> 302 us (level)
  the two profiles are of different devices: /device:TPU:0 before, /device:TPU:19 now
where the time goes in v1:
time: 302 us; the launch traced here: 301 us
  matrix products  105 us (35%)
  waiting for transfers between devices  54.4 us (18%)
  local copies, waits for them, and re-layouts  48.6 us (16%)
  other arithmetic  46.8 us (15%)
  blocking collectives  21.1 us (7%)
  between operations  13.6 us (5%)
  starting transfers between devices  11.9 us (4%)
    ppermute x7, waiting for transfers between devices, swapped_with_each(): part = lax.ppermute(part, axis, [(d, d ^ mask) for d in range(ways)])  54.4 us
    dot_general x2, matrix products, one_block(): lax.dot_general(block_q, block_keys, (((1,), (1,)), ((), ())), preferred_...  44 us
    dot_general x2, matrix products, one_block(): jnp.dot(weights, block_keys[:, :LATENT], preferred_element_type=jnp.float32)  33.3 us
    reduce_sum x2, other arithmetic, one_block(): weights = jax.nn.softmax(scores, axis=-1).astype(jnp.bfloat16)  28 us
    unnamed x12, local copies, waits for them, and re-layouts  14.1 us
    concatenate x1, local copies, waits for them, and re-layouts, body(): jnp.concatenate([latent_q, rotated], axis=-1)  14 us
    all_gather x1, blocking collectives, body(): lax.all_gather(q_low, 'head', axis=1, tiled=True)  13.2 us
    dot_general x1, matrix products, body(): jnp.dot(normed, q_up, preferred_element_type=jnp.float32)  13.2 us
  transfers between devices with their start and end apart: 9, of which 6 were waited for; matrix products, arithmetic and copies ran while one was open for 23% of the time, Pallas kernels for 0%

profile of v1, /device:TPU:19, one launch (start us, length us, event | category | flops | bytes accessed | tf_op | source)
XLA Modules:
  0.0 301.4 jit_solution(4606635840186000333)
XLA Ops:
  8.3 5.6 %all-to-all-start = ((s32[8,1,8]{2,1,0:T(1,128)}), s32[8,1,8]{2,1,0:T(1,128)S(1)}, u32[]{:S(2)}, u32[]{:S(2)}) async-start(s32[8,1,8]{2,1,0:T(1,128)} %bitcast.6), calls=%async_computation | async-start | bytes 8192 | tf_op jit(solution)/shard_map/all_to_all | solution.py:84
  13.9 14.0 %copy.49 = bf16[8192,576]{1,0:T(8,128)(2,1)} copy(bf16[8192,576]{0,1:T(8,128)(2,1)} %param.14) | data formatting | bytes 18874368 | tf_op args[5]
  38.1 3.2 %collective-permute-start.4 = (bf16[1,8,32,576]{3,2,1,0:T(8,128)(2,1)S(1)}, bf16[1,8,32,576]{3,2,1,0:T(8,128)(2,1)S(1)}, u32[]{:S(2)}, u32[]{:S(2)}) collective-permute-start(bf16[1,8,32,576]{3,2,1,0:T(8,128)(2,1)S(1)} %get-tuple-element.44), channel_id=1, source_target_pairs={{0,20},{4,16},{8,28},{12,24},{16,4},{20,0},{24,12},{28,8},{1,21},{... | collective-permute-start | bytes 884744 | tf_op jit(solution)/shard_map/ppermute | solution.py:26
  43.7 11.0 %collective-permute-done.1 = bf16[1,8,32,576]{3,2,1,0:T(8,128)(2,1)S(1)} collective-permute-done((bf16[1,8,32,576]{3,2,1,0:T(8,128)(2,1)S(1)}, bf16[1,8,32,576]{3,2,1,0:T(8,128)(2,1)S(1)}, u32[]{:S(2)}, u32[]{:S(2)}) %collective-permute-start.1) | collective-permute-done | bytes 294944 | tf_op jit(solution)/shard_map/ppermute | solution.py:26
  54.7 7.1 %collective-permute-done.2 = bf16[1,8,32,576]{3,2,1,0:T(8,128)(2,1)S(1)} collective-permute-done((bf16[1,8,32,576]{3,2,1,0:T(8,128)(2,1)S(1)}, bf16[1,8,32,576]{3,2,1,0:T(8,128)(2,1)S(1)}, u32[]{:S(2)}, u32[]{:S(2)}) %collective-permute-start.2) | collective-permute-done | bytes 294944 | tf_op jit(solution)/shard_map/ppermute | solution.py:26
  61.9 3.4 %collective-permute-done.4 = bf16[1,8,32,576]{3,2,1,0:T(8,128)(2,1)S(1)} collective-permute-done((bf16[1,8,32,576]{3,2,1,0:T(8,128)(2,1)S(1)}, bf16[1,8,32,576]{3,2,1,0:T(8,128)(2,1)S(1)}, u32[]{:S(2)}, u32[]{:S(2)}) %collective-permute-start.4) | collective-permute-done | bytes 294944 | tf_op jit(solution)/shard_map/ppermute | solution.py:26
  65.4 23.0 %collective-permute-done.5 = bf16[1,8,32,576]{3,2,1,0:T(8,128)(2,1)S(1)} collective-permute-done((bf16[1,8,32,576]{3,2,1,0:T(8,128)(2,1)S(1)}, bf16[1,8,32,576]{3,2,1,0:T(8,128)(2,1)S(1)}, u32[]{:S(2)}, u32[]{:S(2)}) %collective-permute-start.5) | collective-permute-done | bytes 294944 | tf_op jit(solution)/shard_map/ppermute | solution.py:26
  88.4 7.9 %collective-permute-done.6 = bf16[1,8,32,576]{3,2,1,0:T(8,128)(2,1)S(1)} collective-permute-done((bf16[1,8,32,576]{3,2,1,0:T(8,128)(2,1)S(1)}, bf16[1,8,32,576]{3,2,1,0:T(8,128)(2,1)S(1)}, u32[]{:S(2)}, u32[]{:S(2)}) %collective-permute-start.6) | collective-permute-done | bytes 294944 | tf_op jit(solution)/shard_map/ppermute | solution.py:26
  100.7 7.9 %all-gather = bf16[4,1,384]{2,1,0:T(2,128)(2,1)S(1)} all-gather(bf16[1,1,384]{2,1,0:T(2,128)(2,1)S(1)} %reshape.325), channel_id=1, replica_groups=mesh['seq'=8,'head'=4] {'head'}, dimensions={0}, use_global_device_ids=true | all-gather | bytes 3840 | tf_op jit(solution)/shard_map/all_gather | solution.py:67
  108.7 13.2 %all_gather.9 = bf16[256,1536]{1,0:T(8,128)(2,1)S(1)} all-gather(bf16[256,384]{1,0:T(8,128)(2,1)S(1)} %copy-done.3), channel_id=1, replica_groups=mesh['seq'=8,'head'=4] {'head'}, dimensions={1}, use_global_device_ids=true | all-gather | bytes 983040 | tf_op jit(solution)/shard_map/all_gather | solution.py:66
  122.2 13.2 %convolution_convert_fusion = bf16[256,6144]{1,0:T(8,128)(2,1)} fusion(bf16[1536,6144]{1,0:T(8,128)(2,1)} %param.11, bf16[256,1536]{1,0:T(8,128)(2,1)S(1)} %all_gather.9, f32[1536]{0:T(1024)S(1)} %reshape.327, f32[256]{0:T(256)S(1)} %add_rsqrt_fusion), kind=kOutput, calls=%fused_computation.21 | convolution fusion | flops 4834983936 | bytes 22813696 | tf_op jit(solution)/shard_map/dot_general | solution.py:92
  135.3 3.2 %copy.43 = bf16[256,6144]{0,1:T(8,128)(2,1)S(1)} copy(bf16[256,6144]{1,0:T(8,128)(2,1)} %convolution_convert_fusion) | data formatting | bytes 6291456 | tf_op jit(solution)/shard_map/convert_element_type | solution.py:92
  145.4 4.7 %convert_bitcast_fusion = bf16[256,32,512]{2,0,1:T(8,128)(2,1)S(1)} fusion(bf16[32,128,512]{2,1,0:T(8,128)(2,1)} %param.12, bf16[256,32,192]{0,2,1:T(8,128)(2,1)S(1)} %bitcast.51), kind=kOutput, calls=%fused_computation.20 | convolution fusion | flops 1077936128 | bytes 14680064 | tf_op jit(solution)/shard_map/thn,hnl->thl/dot_general | solution.py:97
  150.1 12.0 %pad_maximum_fusion = bf16[256,32,576]{2,0,1:T(8,128)(2,1)} fusion(bf16[256,32,32]{2,0,1:T(8,128)(2,1)S(1)} %copy-done.2, bf16[256,32,32]{2,0,1:T(8,128)(2,1)S(1)} %copy-done.1, bf16[256,32,512]{2,0,1:T(8,128)(2,1)S(1)} %convert_bitcast_fusion), kind=kLoop, calls=%fused_computation.17 | loop fusion | flops 28311552 | bytes 18874368 | tf_op jit(solution)/shard_map/concatenate | solution.py:100
  162.1 14.0 %copy.47 = bf16[256,32,576]{2,1,0:T(8,128)(2,1)} copy(bf16[256,32,576]{2,0,1:T(8,128)(2,1)} %pad_maximum_fusion) | data formatting | bytes 18874368 | tf_op jit(solution)/shard_map/concatenate | solution.py:100
  176.1 105.9 %while.10 = (s32[]{:T(128)}, bf16[2,4096,512]{2,1,0:T(8,128)(2,1)}, bf16[2,4096,576]{2,1,0:T(8,128)(2,1)}, bf16[2,2048,576]{2,1,0:T(8,128)(2,1)}, s32[]{:T(128)}) while((s32[]{:T(128)}, bf16[2,4096,512]{2,1,0:T(8,128)(2,1)}, bf16[2,4096,576]{2,1,0:T(8,128)(2,1)}, bf16[2,2048,576]{2,1,0:T(8,128)(2,1)}, s32[]{:T(128)}) %tuple.38), condition=%wide.region_6.7_spmd, body=%wide.region_3.6_spmd.sunk | while | flops 18331197440 | bytes 138495600 | solution.py:118
  176.1 22.0 %multiply_reduce_fusion.2 = (f32[4096]{0:T(1024)S(1)}, f32[4096,2048]{0,1:T(8,128)}) fusion(bf16[2,2048,576]{2,1,0:T(8,128)(2,1)} %get-tuple-element.96, s32[]{:T(128)} %get-tuple-element.88, bf16[2,4096,576]{2,1,0:T(8,128)(2,1)} %get-tuple-element.95), kind=kOutput, calls=%fused_computation.4.clone.1 | convolution fusion | flops 9680449536 | bytes 41436160 | tf_op jit(solution)/shard_map/while/body/eval_jaxpr/dot_general | solution.py:108
  198.1 14.0 %fusion.36 = f32[4096]{0:T(1024)S(1)} fusion(f32[4096,2048]{0,1:T(8,128)} %get-tuple-element.81, f32[4096]{0:T(1024)S(1)} %get-tuple-element.82), kind=kLoop, calls=%fused_computation.5.clone.1 | loop fusion | flops 25161728 | bytes 33587200 | tf_op jit(solution)/shard_map/while/body/eval_jaxpr/reduce_sum | solution.py:113
  212.4 16.6 %fusion.37 = bf16[2,4096,512]{2,1,0:T(8,128)(2,1)} fusion(bf16[2,4096,512]{2,1,0:T(8,128)(2,1)} %get-tuple-element.89, s32[]{:T(128)} %get-tuple-element.88, f32[4096,2048]{0,1:T(8,128)} %get-tuple-element.81, f32[4096]{0:T(1024)S(1)} %fusion.36, f32[4096]{0:T(1024)S(1)} %get-tuple-element.82, bf16[2048,576]{1,0:T(8,128)(2,1)S(1)} %dynamic-slice_bitcast_fusion.3), kind=kOutput, calls=%fused_computation.9.clone.1 | convolution fusion | flops 8625586176 | bytes 39879168 | tf_op jit(solution)/shard_map/while/body/eval_jaxpr/dot_general | solution.py:114
  229.0 22.0 %multiply_reduce_fusion.2 = (f32[4096]{0:T(1024)S(1)}, f32[4096,2048]{0,1:T(8,128)}) fusion(bf16[2,2048,576]{2,1,0:T(8,128)(2,1)} %get-tuple-element.96, s32[]{:T(128)} %get-tuple-element.88, bf16[2,4096,576]{2,1,0:T(8,128)(2,1)} %get-tuple-element.95), kind=kOutput, calls=%fused_computation.4.clone.1 | convolution fusion | flops 9680449536 | bytes 41436160 | tf_op jit(solution)/shard_map/while/body/eval_jaxpr/dot_general | solution.py:108
  251.0 14.0 %fusion.36 = f32[4096]{0:T(1024)S(1)} fusion(f32[4096,2048]{0,1:T(8,128)} %get-tuple-element.81, f32[4096]{0:T(1024)S(1)} %get-tuple-element.82), kind=kLoop, calls=%fused_computation.5.clone.1 | loop fusion | flops 25161728 | bytes 33587200 | tf_op jit(solution)/shard_map/while/body/eval_jaxpr/reduce_sum | solution.py:113
  265.3 16.6 %fusion.37 = bf16[2,4096,512]{2,1,0:T(8,128)(2,1)} fusion(bf16[2,4096,512]{2,1,0:T(8,128)(2,1)} %get-tuple-element.89, s32[]{:T(128)} %get-tuple-element.88, f32[4096,2048]{0,1:T(8,128)} %get-tuple-element.81, f32[4096]{0:T(1024)S(1)} %fusion.36, f32[4096]{0:T(1024)S(1)} %get-tuple-element.82, bf16[2048,576]{1,0:T(8,128)(2,1)S(1)} %dynamic-slice_bitcast_fusion.3), kind=kOutput, calls=%fused_computation.9.clone.1 | convolution fusion | flops 8625586176 | bytes 39879168 | tf_op jit(solution)/shard_map/while/body/eval_jaxpr/dot_general | solution.py:114
  281.9 9.7 %fusion.14 = bf16[32,256,128]{1,2,0:T(8,128)(2,1)S(1)} fusion(bf16[32,512,128]{2,1,0:T(8,128)(2,1)} %param.13, bf16[256,32,512]{2,1,0:T(8,128)(2,1)} %bitcast.58), kind=kOutput, calls=%fused_computation.26 | convolution fusion | flops 1074790400 | bytes 14680064 | tf_op jit(solution)/shard_map/thl,hlv->thv/dot_general | solution.py:119
  291.6 2.9 copy.52
  (67 shorter events, 26.5 us)
Async XLA Ops:
  8.3 21.7 %all-to-all-start = ((s32[8,1,8]{2,1,0:T(1,128)}), s32[8,1,8]{2,1,0:T(1,128)S(1)}, u32[]{:S(2)}, u32[]{:S(2)}) async-start(s32[8,1,8]{2,1,0:T(1,128)} %bitcast.6), calls=%async_computation | async-start | bytes 8192 | tf_op jit(solution)/shard_map/all_to_all | solution.py:84
  13.9 162.2 %all-gather.3.cloned.1.call-start = ((), (), s32[]{:S(2)}) async-start(), calls=%async_computation.1 | async-start | bytes 6553600 | tf_op jit(solution)/shard_map/all_gather | solution.py:89
  27.9 2.0 copy-start.5
  35.2 8.1 %collective-permute-start = (bf16[1,8,32,576]{3,2,1,0:T(8,128)(2,1)S(1)}, bf16[1,8,32,576]{3,2,1,0:T(8,128)(2,1)S(1)}, u32[]{:S(2)}, u32[]{:S(2)}) collective-permute-start(bf16[1,8,32,576]{3,2,1,0:T(8,128)(2,1)S(1)} %get-tuple-element.48), channel_id=1, source_target_pairs={{0,4},{4,0},{8,12},{12,8},{16,20},{20,16},{24,28},{28,24},{1,5},{5... | collective-permute-start | bytes 884744 | tf_op jit(solution)/shard_map/ppermute | solution.py:26
  36.5 18.2 %collective-permute-start.1 = (bf16[1,8,32,576]{3,2,1,0:T(8,128)(2,1)S(1)}, bf16[1,8,32,576]{3,2,1,0:T(8,128)(2,1)S(1)}, u32[]{:S(2)}, u32[]{:S(2)}) collective-permute-start(bf16[1,8,32,576]{3,2,1,0:T(8,128)(2,1)S(1)} %get-tuple-element.47), channel_id=1, source_target_pairs={{0,8},{4,12},{8,0},{12,4},{16,24},{20,28},{24,16},{28,20},{1,9},{5... | collective-permute-start | bytes 884744 | tf_op jit(solution)/shard_map/ppermute | solution.py:26
  37.7 24.2 %collective-permute-start.2 = (bf16[1,8,32,576]{3,2,1,0:T(8,128)(2,1)S(1)}, bf16[1,8,32,576]{3,2,1,0:T(8,128)(2,1)S(1)}, u32[]{:S(2)}, u32[]{:S(2)}) collective-permute-start(bf16[1,8,32,576]{3,2,1,0:T(8,128)(2,1)S(1)} %get-tuple-element.46), channel_id=1, source_target_pairs={{0,12},{4,8},{8,4},{12,0},{16,28},{20,24},{24,20},{28,16},{1,13},{... | collective-permute-start | bytes 884744 | tf_op jit(solution)/shard_map/ppermute | solution.py:26
  38.0 23.9 %collective-permute-start.3 = (bf16[1,8,32,576]{3,2,1,0:T(8,128)(2,1)S(1)}, bf16[1,8,32,576]{3,2,1,0:T(8,128)(2,1)S(1)}, u32[]{:S(2)}, u32[]{:S(2)}) collective-permute-start(bf16[1,8,32,576]{3,2,1,0:T(8,128)(2,1)S(1)} %get-tuple-element.45), channel_id=1, source_target_pairs={{0,16},{4,20},{8,24},{12,28},{16,0},{20,4},{24,8},{28,12},{1,17},{... | collective-permute-start | bytes 884744 | tf_op jit(solution)/shard_map/ppermute | solution.py:26
  38.1 27.2 %collective-permute-start.4 = (bf16[1,8,32,576]{3,2,1,0:T(8,128)(2,1)S(1)}, bf16[1,8,32,576]{3,2,1,0:T(8,128)(2,1)S(1)}, u32[]{:S(2)}, u32[]{:S(2)}) collective-permute-start(bf16[1,8,32,576]{3,2,1,0:T(8,128)(2,1)S(1)} %get-tuple-element.44), channel_id=1, source_target_pairs={{0,20},{4,16},{8,28},{12,24},{16,4},{20,0},{24,12},{28,8},{1,21},{... | collective-permute-start | bytes 884744 | tf_op jit(solution)/shard_map/ppermute | solution.py:26
  43.3 45.0 %collective-permute-start.5 = (bf16[1,8,32,576]{3,2,1,0:T(8,128)(2,1)S(1)}, bf16[1,8,32,576]{3,2,1,0:T(8,128)(2,1)S(1)}, u32[]{:S(2)}, u32[]{:S(2)}) collective-permute-start(bf16[1,8,32,576]{3,2,1,0:T(8,128)(2,1)S(1)} %get-tuple-element.43), channel_id=1, source_target_pairs={{0,24},{4,28},{8,16},{12,20},{16,8},{20,12},{24,0},{28,4},{1,25},{... | collective-permute-start | bytes 884744 | tf_op jit(solution)/shard_map/ppermute | solution.py:26
  54.7 41.6 %collective-permute-start.6 = (bf16[1,8,32,576]{3,2,1,0:T(8,128)(2,1)S(1)}, bf16[1,8,32,576]{3,2,1,0:T(8,128)(2,1)S(1)}, u32[]{:S(2)}, u32[]{:S(2)}) collective-permute-start(bf16[1,8,32,576]{3,2,1,0:T(8,128)(2,1)S(1)} %get-tuple-element.42), channel_id=1, source_target_pairs={{0,28},{4,24},{8,20},{12,16},{16,12},{20,8},{24,4},{28,0},{1,29},{... | collective-permute-start | bytes 884744 | tf_op jit(solution)/shard_map/ppermute | solution.py:26
  96.3 4.4 %copy-start.4 = (bf16[384]{0:T(512)(128)(2,1)S(1)}, bf16[384]{0:T(512)(128)(2,1)}, u32[]{:S(2)}) copy-start(bf16[384]{0:T(512)(128)(2,1)} %param.10) | copy-start | bytes 2308
  96.3 12.4 %copy-start.3 = (bf16[256,384]{1,0:T(8,128)(2,1)S(1)}, bf16[256,384]{1,0:T(8,128)(2,1)}, u32[]{:S(2)}) copy-start(bf16[256,384]{1,0:T(8,128)(2,1)} %param.9) | copy-start | bytes 589828
  145.4 4.7 %copy-start.1 = (bf16[256,32,32]{2,0,1:T(8,128)(2,1)S(1)}, bf16[256,32,32]{2,0,1:T(8,128)(2,1)}, u32[]{:S(2)}) copy-start(bf16[256,32,32]{2,0,1:T(8,128)(2,1)} %copy.45) | copy-start | bytes 1572868
  145.4 4.7 %copy-start.2 = (bf16[256,32,32]{2,0,1:T(8,128)(2,1)S(1)}, bf16[256,32,32]{2,0,1:T(8,128)(2,1)}, u32[]{:S(2)}) copy-start(bf16[256,32,32]{2,0,1:T(8,128)(2,1)} %copy.46) | copy-start | bytes 1572868
  198.1 14.0 %copy-start = (bf16[2,2048,576]{2,1,0:T(8,128)(2,1)S(1)}, bf16[2,2048,576]{2,1,0:T(8,128)(2,1)}, u32[]{:S(2)}) copy-start(bf16[2,2048,576]{2,1,0:T(8,128)(2,1)} %get-tuple-element.96) | copy-start | bytes 14155780 | tf_op jit(solution)/shard_map/while
  251.0 14.0 %copy-start = (bf16[2,2048,576]{2,1,0:T(8,128)(2,1)S(1)}, bf16[2,2048,576]{2,1,0:T(8,128)(2,1)}, u32[]{:S(2)}) copy-start(bf16[2,2048,576]{2,1,0:T(8,128)(2,1)} %get-tuple-element.96) | copy-start | bytes 14155780 | tf_op jit(solution)/shard_map/while
Sparse Core Ops, SparseCore 0:
  100.8 45.3 all-gather.2
